TPU v7x, 32 devices: a whole 2x2x4 slice. The times are simulated.
32 devices in a mesh: sec: 4 (over y, x), bond: 8 (over z, core).
Axes of the slice: x: 2, y: 2, z: 4, core: 2. Of those that a mesh axis runs over, the one named last changes fastest.
Arguments:
- left_vectors: bfloat16 [128, 4096], P(None, 'bond'), may hold values from -6 to 6
- site_tensors: bfloat16 [4, 4096, 4, 4096], P('sec', None, None, 'bond'), may hold values from -0.09375 to 0.09375
- displacement: float32 [128, 216], P('sec'), may hold values from -2.5 to 2.5
- photon_counts: int32 [128, 216], P('sec'), may hold values from 0 to 3
- mode_order: int32 [216], replicated, may hold values from 0 to 215, each once
Outputs:
- log_likelihood: float32 [4, 128], P('sec')
- log_norm: float32 [4, 128], P('sec')
Inputs may be any that keep to these rules, and one draw needn't show every extreme that they name: `mode_order`: each of the 216 modes appears once.
All inputs are finite; a program needn't handle non-finite values.
Results may differ from a plain program's by a relative error of at most 0.0015.
Values may be sent and summed in bfloat16 or wider, within the bound.
No kernel may reach another device: no remote copies, remote signals or barrier semaphores. Data moves between devices by JAX's collectives and lax.ppermute only.
A program may use at most 64 MiB of HBM per device.

v0:
```python
import math
import jax
import jax.numpy as jnp
from jax import lax
from jax.sharding import PartitionSpec as P

CUT = 4
epsilon = 1e-06


def passed_along(x, axis, by):
    size = lax.axis_size(axis)
    pairs = [(i, i + by) for i in range(size) if 0 <= i + by < size]
    return lax.ppermute(x, axis, pairs)


def displacement_table(cutoff):
    table = [
        [[0.0 for degree_slot in range(2 * cutoff - 1)] for col_level in range(cutoff)]
        for row_level in range(cutoff)
    ]
    for row_level in range(cutoff):
        for col_level in range(cutoff):
            lower = min(row_level, col_level)
            upper = max(row_level, col_level)
            excess = upper - lower
            parity = 1.0 if row_level >= col_level else (-1.0) ** excess
            prefactor = math.sqrt(math.factorial(lower) / math.factorial(upper))
            for term in range(lower + 1):
                table[row_level][col_level][excess + 2 * term] += (
                    parity
                    * prefactor
                    * (-1.0) ** term
                    * math.comb(upper, lower - term)
                    / math.factorial(term)
                )
    return table


def displacement_matrix(amplitude):
    table = jnp.asarray(displacement_table(CUT), dtype=jnp.float32)
    power_list = [jnp.ones_like(amplitude)]
    for degree in range(2 * CUT - 2):
        power_list.append(power_list[-1] * amplitude)
    power_stack = jnp.stack(power_list, axis=1)
    poly = jnp.einsum("sp,mnp->smn", power_stack, table, precision=lax.Precision.HIGHEST)
    return jnp.exp(-0.5 * amplitude * amplitude)[:, None, None] * poly


def local(left_vectors, site_tensors, displacement, photon_counts, mode_order):
    full_width = site_tensors.shape[1]
    cutoff = site_tensors.shape[2]
    local_width = site_tensors.shape[3]
    samples = left_vectors.shape[0]
    segment_count = lax.axis_size("sec")
    segment_index = lax.axis_index("sec")
    matrix = site_tensors.reshape(full_width, cutoff * local_width)
    stacked = jnp.stack([displacement, photon_counts.astype(jnp.float32)])
    mode_total = displacement.shape[1]
    window_order = mode_order[:segment_count]
    picker = (window_order[None, :] == jnp.arange(mode_total, dtype=jnp.int32)[:, None]).astype(
        jnp.float32
    )
    ordered = jnp.einsum("rsm,mj->rsj", stacked, picker, precision=lax.Precision.HIGHEST)
    columns = lax.all_to_all(ordered, "sec", split_axis=2, concat_axis=1, tiled=True)
    matrices_all = displacement_matrix(columns[0, :, 0])
    counts_all = columns[1, :, 0]
    levels = jnp.arange(cutoff).astype(jnp.float32)
    blocks = 4
    block_rows = samples // blocks
    incoming_zero = jnp.zeros((block_rows, local_width), jnp.float32)
    extra_zero = jnp.zeros((block_rows,), jnp.float32)

    def add_rows(fragment):
        return jnp.dot(fragment, matrix, preferred_element_type=jnp.float32)

    def one_step(turn_index, state):
        incoming, extra_in, record, norm_record = state
        block_index = turn_index - segment_index
        usable = (block_index >= 0) & (block_index < blocks)
        clamped = jnp.clip(block_index, 0, blocks - 1)
        first_row = clamped * block_rows
        opening = lax.dynamic_slice_in_dim(left_vectors, first_row, block_rows, 0)
        source = jnp.where(segment_index == 0, opening, incoming.astype(jnp.bfloat16))
        factor = jnp.where(segment_index == 0, jnp.ones_like(extra_in), extra_in)
        projected = add_rows(lax.all_gather(source, "bond", axis=1, tiled=True))
        projected = (projected * factor[:, None]).reshape(block_rows, cutoff, local_width)
        shifts = lax.dynamic_slice_in_dim(matrices_all, first_row, block_rows, 0)
        counted = lax.dynamic_slice_in_dim(counts_all, first_row, block_rows, 0)
        displaced = jnp.einsum("smn,snb->smb", shifts, projected, precision=lax.Precision.HIGHEST)
        partial_value = jnp.sum(displaced * displaced, axis=2)
        weights = lax.psum(partial_value, "bond")
        select = (counted[:, None] == levels[None, :]).astype(jnp.float32)
        chosen_weight = jnp.sum(select * weights, axis=1)
        log_prob = jnp.log(chosen_weight) - jnp.log(jnp.sum(weights, axis=1))
        log_scale = jnp.log(chosen_weight / full_width + epsilon)
        chosen = jnp.sum(select[:, :, None] * displaced, axis=1)
        next_vector = chosen.astype(jnp.bfloat16)
        previous = lax.dynamic_slice_in_dim(record, first_row, block_rows, 0)
        record = lax.dynamic_update_slice_in_dim(
            record, jnp.where(usable, log_prob, previous), first_row, 0
        )
        previous_norm = lax.dynamic_slice_in_dim(norm_record, first_row, block_rows, 0)
        norm_record = lax.dynamic_update_slice_in_dim(
            norm_record, jnp.where(usable, log_scale, previous_norm), first_row, 0
        )
        extra_out = lax.rsqrt(chosen_weight / full_width + epsilon)
        incoming, extra_next = passed_along((next_vector.astype(jnp.float32), extra_out), "sec", 1)
        return (incoming, extra_next, record, norm_record)

    record_zero = jnp.zeros((samples,), jnp.float32)
    final_state = lax.fori_loop(
        0,
        segment_count + blocks - 1,
        one_step,
        (incoming_zero, extra_zero, record_zero, record_zero),
    )
    return (final_state[2][None, :], final_state[3][None, :])


def solution(mesh):
    placed = (P(None, "bond"), P("sec", None, None, "bond"), P("sec", None), P("sec", None), P())
    return jax.shard_map(
        local,
        mesh=mesh,
        in_specs=placed,
        out_specs=(P("sec", None), P("sec", None)),
        check_vma=False,
    )
```

profile of v0, /device:TPU:0, one launch (start us, length us, event | category | flops | bytes accessed | tf_op | source)
XLA Modules:
  0.0 450.2 jit_solution(1115947929308692932)
XLA Ops:
  2.1 0.9 fusion.6
  3.7 5.2 %all-to-all-start = ((f32[2,32,4]{1,0,2:T(2,128)}), f32[2,32,4]{1,0,2:T(2,128)S(1)}, u32[]{:S(2)}, u32[]{:S(2)}) async-start(f32[2,32,4]{1,0,2:T(2,128)} %copy.9), calls=%async_computation | async-start | bytes 8192 | tf_op jit(solution)/shard_map/all_to_all | solution.py:65
  8.8 16.9 %copy.12 = bf16[512,8,4,512]{3,1,2,0:T(8,128)(2,1)} copy(bf16[512,8,4,512]{3,2,1,0:T(4,128)(2,1)} %bitcast.32) | data formatting | bytes 33554432
  26.3 423.5 %while.21 = (s32[]{:T(128)}, bf16[32,512]{1,0:T(8,128)(2,1)S(1)}, f32[32]{0:T(128)S(1)}, f32[128]{0:T(128)S(1)}, f32[128]{0:T(128)S(1)}, /*index=5*/s32[]{:T(128...) while((s32[]{:T(128)}, bf16[32,512]{1,0:T(8,128)(2,1)S(1)}, ...), condition=%wide.region_6.7_spmd.clone, body=%wide.region_0.6_spmd.clone.sunk | while | flops 540345216 | bytes 18662804 | solution.py:112
  27.1 14.4 %all_gather.10 = bf16[32,4096]{1,0:T(8,128)(2,1)S(1)} all-gather(bf16[32,512]{1,0:T(8,128)(2,1)S(1)} %convert_select_fusion.2), channel_id=1, replica_groups=mesh['sec'=4,'bond'=8] {'bond'}, dimensions={1}, use_global_device_ids=true | all-gather | bytes 294912 | tf_op jit(solution)/shard_map/while/body/eval_jaxpr/all_gather | solution.py:86
  41.5 8.8 %convolution_multiply_fusion.3 = f32[32,2048]{1,0:T(8,128)S(1)} fusion(bf16[32,4096]{1,0:T(8,128)(2,1)S(1)} %all_gather.10, bf16[4096,2048]{1,0:T(8,128)(2,1)} %get-tuple-element.446, f32[32]{0:T(128)S(1)} %broadcast_select_fusion.4), kind=kOutput, calls=%fused_computation.1.clone.1 | convolution fusion | flops 536936448 | bytes 17301632 | tf_op jit(solution)/shard_map/while/body/eval_jaxpr/dot_general | solution.py:75
  50.8 0.8 multiply_reduce_fusion.3
  51.6 3.9 collective-permute-start
  55.6 28.8 %psum.14 = f32[32,4]{1,0:T(8,128)S(1)} all-reduce(f32[32,4]{1,0:T(8,128)S(1)} %get-tuple-element.396), channel_id=1, replica_groups=mesh['sec'=4,'bond'=8] {'bond'}, use_global_device_ids=true, to_apply=%region_3.3 | all-reduce | flops 128 | bytes 1024 | tf_op jit(solution)/shard_map/while/body/eval_jaxpr/psum | solution.py:92
  84.8 3.4 collective-permute-start.1
  88.1 1.3 collective-permute-done.1
  90.2 14.2 %all_gather.10 = bf16[32,4096]{1,0:T(8,128)(2,1)S(1)} all-gather(bf16[32,512]{1,0:T(8,128)(2,1)S(1)} %convert_select_fusion.2), channel_id=1, replica_groups=mesh['sec'=4,'bond'=8] {'bond'}, dimensions={1}, use_global_device_ids=true | all-gather | bytes 294912 | tf_op jit(solution)/shard_map/while/body/eval_jaxpr/all_gather | solution.py:86
  104.4 8.8 %convolution_multiply_fusion.3 = f32[32,2048]{1,0:T(8,128)S(1)} fusion(bf16[32,4096]{1,0:T(8,128)(2,1)S(1)} %all_gather.10, bf16[4096,2048]{1,0:T(8,128)(2,1)} %get-tuple-element.446, f32[32]{0:T(128)S(1)} %broadcast_select_fusion.4), kind=kOutput, calls=%fused_computation.1.clone.1 | convolution fusion | flops 536936448 | bytes 17301632 | tf_op jit(solution)/shard_map/while/body/eval_jaxpr/dot_general | solution.py:75
  114.5 4.2 collective-permute-start
  118.7 25.9 %psum.14 = f32[32,4]{1,0:T(8,128)S(1)} all-reduce(f32[32,4]{1,0:T(8,128)S(1)} %get-tuple-element.396), channel_id=1, replica_groups=mesh['sec'=4,'bond'=8] {'bond'}, use_global_device_ids=true, to_apply=%region_3.3 | all-reduce | flops 128 | bytes 1024 | tf_op jit(solution)/shard_map/while/body/eval_jaxpr/psum | solution.py:92
  145.0 4.3 collective-permute-start.1
  149.2 1.3 collective-permute-done.1
  151.3 14.2 %all_gather.10 = bf16[32,4096]{1,0:T(8,128)(2,1)S(1)} all-gather(bf16[32,512]{1,0:T(8,128)(2,1)S(1)} %convert_select_fusion.2), channel_id=1, replica_groups=mesh['sec'=4,'bond'=8] {'bond'}, dimensions={1}, use_global_device_ids=true | all-gather | bytes 294912 | tf_op jit(solution)/shard_map/while/body/eval_jaxpr/all_gather | solution.py:86
  165.5 8.8 %convolution_multiply_fusion.3 = f32[32,2048]{1,0:T(8,128)S(1)} fusion(bf16[32,4096]{1,0:T(8,128)(2,1)S(1)} %all_gather.10, bf16[4096,2048]{1,0:T(8,128)(2,1)} %get-tuple-element.446, f32[32]{0:T(128)S(1)} %broadcast_select_fusion.4), kind=kOutput, calls=%fused_computation.1.clone.1 | convolution fusion | flops 536936448 | bytes 17301632 | tf_op jit(solution)/shard_map/while/body/eval_jaxpr/dot_general | solution.py:75
  175.6 4.2 collective-permute-start
  179.8 25.9 %psum.14 = f32[32,4]{1,0:T(8,128)S(1)} all-reduce(f32[32,4]{1,0:T(8,128)S(1)} %get-tuple-element.396), channel_id=1, replica_groups=mesh['sec'=4,'bond'=8] {'bond'}, use_global_device_ids=true, to_apply=%region_3.3 | all-reduce | flops 128 | bytes 1024 | tf_op jit(solution)/shard_map/while/body/eval_jaxpr/psum | solution.py:92
  206.0 3.0 collective-permute-start.1
  209.1 1.3 collective-permute-done.1
  211.1 14.2 %all_gather.10 = bf16[32,4096]{1,0:T(8,128)(2,1)S(1)} all-gather(bf16[32,512]{1,0:T(8,128)(2,1)S(1)} %convert_select_fusion.2), channel_id=1, replica_groups=mesh['sec'=4,'bond'=8] {'bond'}, dimensions={1}, use_global_device_ids=true | all-gather | bytes 294912 | tf_op jit(solution)/shard_map/while/body/eval_jaxpr/all_gather | solution.py:86
  225.3 8.8 %convolution_multiply_fusion.3 = f32[32,2048]{1,0:T(8,128)S(1)} fusion(bf16[32,4096]{1,0:T(8,128)(2,1)S(1)} %all_gather.10, bf16[4096,2048]{1,0:T(8,128)(2,1)} %get-tuple-element.446, f32[32]{0:T(128)S(1)} %broadcast_select_fusion.4), kind=kOutput, calls=%fused_computation.1.clone.1 | convolution fusion | flops 536936448 | bytes 17301632 | tf_op jit(solution)/shard_map/while/body/eval_jaxpr/dot_general | solution.py:75
  235.4 4.2 collective-permute-start
  239.6 25.9 %psum.14 = f32[32,4]{1,0:T(8,128)S(1)} all-reduce(f32[32,4]{1,0:T(8,128)S(1)} %get-tuple-element.396), channel_id=1, replica_groups=mesh['sec'=4,'bond'=8] {'bond'}, use_global_device_ids=true, to_apply=%region_3.3 | all-reduce | flops 128 | bytes 1024 | tf_op jit(solution)/shard_map/while/body/eval_jaxpr/psum | solution.py:92
  265.9 3.0 collective-permute-start.1
  268.9 1.3 collective-permute-done.1
  271.0 14.2 %all_gather.10 = bf16[32,4096]{1,0:T(8,128)(2,1)S(1)} all-gather(bf16[32,512]{1,0:T(8,128)(2,1)S(1)} %convert_select_fusion.2), channel_id=1, replica_groups=mesh['sec'=4,'bond'=8] {'bond'}, dimensions={1}, use_global_device_ids=true | all-gather | bytes 294912 | tf_op jit(solution)/shard_map/while/body/eval_jaxpr/all_gather | solution.py:86
  285.2 8.8 %convolution_multiply_fusion.3 = f32[32,2048]{1,0:T(8,128)S(1)} fusion(bf16[32,4096]{1,0:T(8,128)(2,1)S(1)} %all_gather.10, bf16[4096,2048]{1,0:T(8,128)(2,1)} %get-tuple-element.446, f32[32]{0:T(128)S(1)} %broadcast_select_fusion.4), kind=kOutput, calls=%fused_computation.1.clone.1 | convolution fusion | flops 536936448 | bytes 17301632 | tf_op jit(solution)/shard_map/while/body/eval_jaxpr/dot_general | solution.py:75
  294.4 0.8 multiply_reduce_fusion.3
  295.3 4.2 collective-permute-start
  299.4 25.9 %psum.14 = f32[32,4]{1,0:T(8,128)S(1)} all-reduce(f32[32,4]{1,0:T(8,128)S(1)} %get-tuple-element.396), channel_id=1, replica_groups=mesh['sec'=4,'bond'=8] {'bond'}, use_global_device_ids=true, to_apply=%region_3.3 | all-reduce | flops 128 | bytes 1024 | tf_op jit(solution)/shard_map/while/body/eval_jaxpr/psum | solution.py:92
  325.7 3.0 collective-permute-start.1
  328.8 1.3 collective-permute-done.1
  330.8 14.2 %all_gather.10 = bf16[32,4096]{1,0:T(8,128)(2,1)S(1)} all-gather(bf16[32,512]{1,0:T(8,128)(2,1)S(1)} %convert_select_fusion.2), channel_id=1, replica_groups=mesh['sec'=4,'bond'=8] {'bond'}, dimensions={1}, use_global_device_ids=true | all-gather | bytes 294912 | tf_op jit(solution)/shard_map/while/body/eval_jaxpr/all_gather | solution.py:86
  345.0 8.8 %convolution_multiply_fusion.3 = f32[32,2048]{1,0:T(8,128)S(1)} fusion(bf16[32,4096]{1,0:T(8,128)(2,1)S(1)} %all_gather.10, bf16[4096,2048]{1,0:T(8,128)(2,1)} %get-tuple-element.446, f32[32]{0:T(128)S(1)} %broadcast_select_fusion.4), kind=kOutput, calls=%fused_computation.1.clone.1 | convolution fusion | flops 536936448 | bytes 17301632 | tf_op jit(solution)/shard_map/while/body/eval_jaxpr/dot_general | solution.py:75
  355.1 4.2 collective-permute-start
  359.3 25.9 %psum.14 = f32[32,4]{1,0:T(8,128)S(1)} all-reduce(f32[32,4]{1,0:T(8,128)S(1)} %get-tuple-element.396), channel_id=1, replica_groups=mesh['sec'=4,'bond'=8] {'bond'}, use_global_device_ids=true, to_apply=%region_3.3 | all-reduce | flops 128 | bytes 1024 | tf_op jit(solution)/shard_map/while/body/eval_jaxpr/psum | solution.py:92
  385.6 3.0 collective-permute-start.1
  388.6 1.3 collective-permute-done.1
  390.6 14.2 %all_gather.10 = bf16[32,4096]{1,0:T(8,128)(2,1)S(1)} all-gather(bf16[32,512]{1,0:T(8,128)(2,1)S(1)} %convert_select_fusion.2), channel_id=1, replica_groups=mesh['sec'=4,'bond'=8] {'bond'}, dimensions={1}, use_global_device_ids=true | all-gather | bytes 294912 | tf_op jit(solution)/shard_map/while/body/eval_jaxpr/all_gather | solution.py:86
  404.8 8.8 %convolution_multiply_fusion.3 = f32[32,2048]{1,0:T(8,128)S(1)} fusion(bf16[32,4096]{1,0:T(8,128)(2,1)S(1)} %all_gather.10, bf16[4096,2048]{1,0:T(8,128)(2,1)} %get-tuple-element.446, f32[32]{0:T(128)S(1)} %broadcast_select_fusion.4), kind=kOutput, calls=%fused_computation.1.clone.1 | convolution fusion | flops 536936448 | bytes 17301632 | tf_op jit(solution)/shard_map/while/body/eval_jaxpr/dot_general | solution.py:75
  414.9 4.2 collective-permute-start
  419.1 25.9 %psum.14 = f32[32,4]{1,0:T(8,128)S(1)} all-reduce(f32[32,4]{1,0:T(8,128)S(1)} %get-tuple-element.396), channel_id=1, replica_groups=mesh['sec'=4,'bond'=8] {'bond'}, use_global_device_ids=true, to_apply=%region_3.3 | all-reduce | flops 128 | bytes 1024 | tf_op jit(solution)/shard_map/while/body/eval_jaxpr/psum | solution.py:92
  445.4 3.0 collective-permute-start.1
  448.4 1.3 collective-permute-done.1
  (105 shorter events, 18.7 us)
Async XLA Ops:
  3.7 22.1 %all-to-all-start = ((f32[2,32,4]{1,0,2:T(2,128)}), f32[2,32,4]{1,0,2:T(2,128)S(1)}, u32[]{:S(2)}, u32[]{:S(2)}) async-start(f32[2,32,4]{1,0,2:T(2,128)} %copy.9), calls=%async_computation | async-start | bytes 8192 | tf_op jit(solution)/shard_map/all_to_all | solution.py:65
  8.8 17.2 %copy-start.2 = (f32[4,4,7]{2,1,0:T(4,128)S(1)}, f32[4,4,7]{2,1,0:T(4,128)}, u32[]{:S(2)}) copy-start(f32[4,4,7]{2,1,0:T(4,128)} %constant.99.clone) | copy-start | bytes 1348
  51.6 37.8 %collective-permute-start = (bf16[32,512]{1,0:T(8,128)(2,1)S(1)}, bf16[32,512]{1,0:T(8,128)(2,1)S(1)}, u32[]{:S(2)}, u32[]{:S(2)}) collective-permute-start(bf16[32,512]{1,0:T(8,128)(2,1)S(1)} %get-tuple-element.395), channel_id=1, source_target_pairs={{0,8},{8,16},{16,24},{1,9},{9,17},{17,25},{2,10},{10,18},{18,26},{... | collective-permute-start | bytes 98312 | tf_op jit(solution)/shard_map/while/body/eval_jaxpr/ppermute | solution.py:14
  84.8 4.7 %collective-permute-start.1 = (f32[32]{0:T(128)S(1)}, f32[32]{0:T(128)S(1)}, u32[]{:S(2)}, u32[]{:S(2)}) collective-permute-start(f32[32]{0:T(128)S(1)} %get-tuple-element.399), channel_id=1, source_target_pairs={{0,8},{8,16},{16,24},{1,9},{9,17},{17,25},{2,10},{10,18},{18,26},{... | collective-permute-start | bytes 392 | tf_op jit(solution)/shard_map/while/body/eval_jaxpr/ppermute | solution.py:14
  114.5 36.0 %collective-permute-start = (bf16[32,512]{1,0:T(8,128)(2,1)S(1)}, bf16[32,512]{1,0:T(8,128)(2,1)S(1)}, u32[]{:S(2)}, u32[]{:S(2)}) collective-permute-start(bf16[32,512]{1,0:T(8,128)(2,1)S(1)} %get-tuple-element.395), channel_id=1, source_target_pairs={{0,8},{8,16},{16,24},{1,9},{9,17},{17,25},{2,10},{10,18},{18,26},{... | collective-permute-start | bytes 98312 | tf_op jit(solution)/shard_map/while/body/eval_jaxpr/ppermute | solution.py:14
  145.0 5.5 %collective-permute-start.1 = (f32[32]{0:T(128)S(1)}, f32[32]{0:T(128)S(1)}, u32[]{:S(2)}, u32[]{:S(2)}) collective-permute-start(f32[32]{0:T(128)S(1)} %get-tuple-element.399), channel_id=1, source_target_pairs={{0,8},{8,16},{16,24},{1,9},{9,17},{17,25},{2,10},{10,18},{18,26},{... | collective-permute-start | bytes 392 | tf_op jit(solution)/shard_map/while/body/eval_jaxpr/ppermute | solution.py:14
  175.6 34.8 %collective-permute-start = (bf16[32,512]{1,0:T(8,128)(2,1)S(1)}, bf16[32,512]{1,0:T(8,128)(2,1)S(1)}, u32[]{:S(2)}, u32[]{:S(2)}) collective-permute-start(bf16[32,512]{1,0:T(8,128)(2,1)S(1)} %get-tuple-element.395), channel_id=1, source_target_pairs={{0,8},{8,16},{16,24},{1,9},{9,17},{17,25},{2,10},{10,18},{18,26},{... | collective-permute-start | bytes 98312 | tf_op jit(solution)/shard_map/while/body/eval_jaxpr/ppermute | solution.py:14
  206.0 4.3 collective-permute-start.1
  235.4 34.8 %collective-permute-start = (bf16[32,512]{1,0:T(8,128)(2,1)S(1)}, bf16[32,512]{1,0:T(8,128)(2,1)S(1)}, u32[]{:S(2)}, u32[]{:S(2)}) collective-permute-start(bf16[32,512]{1,0:T(8,128)(2,1)S(1)} %get-tuple-element.395), channel_id=1, source_target_pairs={{0,8},{8,16},{16,24},{1,9},{9,17},{17,25},{2,10},{10,18},{18,26},{... | collective-permute-start | bytes 98312 | tf_op jit(solution)/shard_map/while/body/eval_jaxpr/ppermute | solution.py:14
  265.9 4.3 collective-permute-start.1
  295.3 34.8 %collective-permute-start = (bf16[32,512]{1,0:T(8,128)(2,1)S(1)}, bf16[32,512]{1,0:T(8,128)(2,1)S(1)}, u32[]{:S(2)}, u32[]{:S(2)}) collective-permute-start(bf16[32,512]{1,0:T(8,128)(2,1)S(1)} %get-tuple-element.395), channel_id=1, source_target_pairs={{0,8},{8,16},{16,24},{1,9},{9,17},{17,25},{2,10},{10,18},{18,26},{... | collective-permute-start | bytes 98312 | tf_op jit(solution)/shard_map/while/body/eval_jaxpr/ppermute | solution.py:14
  325.7 4.3 collective-permute-start.1
  355.1 34.8 %collective-permute-start = (bf16[32,512]{1,0:T(8,128)(2,1)S(1)}, bf16[32,512]{1,0:T(8,128)(2,1)S(1)}, u32[]{:S(2)}, u32[]{:S(2)}) collective-permute-start(bf16[32,512]{1,0:T(8,128)(2,1)S(1)} %get-tuple-element.395), channel_id=1, source_target_pairs={{0,8},{8,16},{16,24},{1,9},{9,17},{17,25},{2,10},{10,18},{18,26},{... | collective-permute-start | bytes 98312 | tf_op jit(solution)/shard_map/while/body/eval_jaxpr/ppermute | solution.py:14
  385.6 4.3 collective-permute-start.1
  414.9 34.8 %collective-permute-start = (bf16[32,512]{1,0:T(8,128)(2,1)S(1)}, bf16[32,512]{1,0:T(8,128)(2,1)S(1)}, u32[]{:S(2)}, u32[]{:S(2)}) collective-permute-start(bf16[32,512]{1,0:T(8,128)(2,1)S(1)} %get-tuple-element.395), channel_id=1, source_target_pairs={{0,8},{8,16},{16,24},{1,9},{9,17},{17,25},{2,10},{10,18},{18,26},{... | collective-permute-start | bytes 98312 | tf_op jit(solution)/shard_map/while/body/eval_jaxpr/ppermute | solution.py:14
  445.4 4.3 collective-permute-start.1
  449.7 0.5 copy-start
  449.7 0.5 copy-start.1
where the time goes:
time: 452 us; the launch traced here: 450 us
  blocking collectives  284 us (63%)
  matrix products  68 us (15%)
  starting transfers between devices  56.8 us (13%)
  local copies, waits for them, and re-layouts  22.2 us (5%)
  other arithmetic  9.19 us (2%)
  waiting for transfers between devices  8.94 us (2%)
    psum x7, blocking collectives, one_step(): weights = lax.psum(partial_value, 'bond')  184 us
    all_gather x7, blocking collectives, one_step(): projected = add_rows(lax.all_gather(source, 'bond', axis=1, tiled=True))  99.6 us
    dot_general x7, matrix products, add_rows(): return jnp.dot(fragment, matrix, preferred_element_type=jnp.float32)  61.3 us
    ppermute x14, starting transfers between devices, passed_along(): return lax.ppermute(x, axis, pairs)  51.6 us
    unnamed x7, local copies, waits for them, and re-layouts  17.4 us
  transfers between devices with their start and end apart: 15, of which 7 were waited for; matrix products, arithmetic and copies ran while one was open for 4% of the time, Pallas kernels for 0%

commit v1 on v0

--- a/solution.py
+++ b/solution.py
@@ -89,7 +89,8 @@
         counted = lax.dynamic_slice_in_dim(counts_all, first_row, block_rows, 0)
         displaced = jnp.einsum("smn,snb->smb", shifts, projected, precision=lax.Precision.HIGHEST)
         partial_value = jnp.sum(displaced * displaced, axis=2)
-        weights = lax.psum(partial_value, "bond")
+        squares_do = lambda view, across: jnp.sum(lax.all_gather(view, across), axis=0)
+        weights = squares_do(partial_value, "bond")
         select = (counted[:, None] == levels[None, :]).astype(jnp.float32)
         chosen_weight = jnp.sum(select * weights, axis=1)
         log_prob = jnp.log(chosen_weight) - jnp.log(jnp.sum(weights, axis=1))

time: 452 us -> 356 us (0.79)
  blocking collectives: 284 us -> 189 us
    psum x7 -> x0, blocking collectives: 184 us -> none  [one_step(): weights = lax.psum(partial_value, 'bond')]
    all_gather x0 -> x7, blocking collectives: none -> 89.4 us  [one_step(): lax.all_gather(view, across)]
  transfers between devices with their start and end apart: 15 -> 15, of which waited for: 7 -> 7; matrix products, arithmetic and copies ran while one was open for 4% -> 5% of each run, Pallas kernels for 0% -> 0%
where the time goes in v1:
time: 356 us; the launch traced here: 355 us
  blocking collectives  189 us (53%)
  matrix products  68.1 us (19%)
  starting transfers between devices  55.8 us (16%)
  local copies, waits for them, and re-layouts  23.4 us (7%)
  waiting for transfers between devices  8.94 us (3%)
  other arithmetic  8.62 us (2%)
    all_gather x7, blocking collectives, one_step(): projected = add_rows(lax.all_gather(source, 'bond', axis=1, tiled=True))  99.6 us
    all_gather x7, blocking collectives, one_step(): lax.all_gather(view, across)  89.4 us
    dot_general x7, matrix products, add_rows(): return jnp.dot(fragment, matrix, preferred_element_type=jnp.float32)  61.3 us
    ppermute x14, starting transfers between devices, passed_along(): return lax.ppermute(x, axis, pairs)  50.6 us
    unnamed x7, local copies, waits for them, and re-layouts  17.4 us
    ppermute x14, waiting for transfers between devices, passed_along(): return lax.ppermute(x, axis, pairs)  8.93 us
  transfers between devices with their start and end apart: 15, of which 7 were waited for; matrix products, arithmetic and copies ran while one was open for 5% of the time, Pallas kernels for 0%

profile of v1, /device:TPU:0, one launch (start us, length us, event | category | flops | bytes accessed | tf_op | source)
XLA Modules:
  0.0 354.8 jit_solution(5637536636743607543)
XLA Ops:
  2.1 0.9 fusion.6
  3.7 5.2 %all-to-all-start = ((f32[2,32,4]{1,0,2:T(2,128)}), f32[2,32,4]{1,0,2:T(2,128)S(1)}, u32[]{:S(2)}, u32[]{:S(2)}) async-start(f32[2,32,4]{1,0,2:T(2,128)} %copy.11), calls=%async_computation | async-start | bytes 8192 | tf_op jit(solution)/shard_map/all_to_all | solution.py:65
  8.8 16.9 %copy.14 = bf16[512,8,4,512]{3,1,2,0:T(8,128)(2,1)} copy(bf16[512,8,4,512]{3,2,1,0:T(4,128)(2,1)} %bitcast.35) | data formatting | bytes 33554432
  26.3 328.0 %while.21 = (s32[]{:T(128)}, bf16[32,512]{1,0:T(8,128)(2,1)S(1)}, f32[32]{0:T(128)S(1)}, f32[128]{0:T(128)S(1)}, f32[128]{0:T(128)S(1)}, /*index=5*/s32[]{:T(128...) while((s32[]{:T(128)}, bf16[32,512]{1,0:T(8,128)(2,1)S(1)}, ...), condition=%wide.region_6.7_spmd.clone, body=%wide.region_0.6_spmd.clone.sunk | while | flops 540346880 | bytes 18673044 | solution.py:113
  27.1 14.4 %all_gather.26 = bf16[32,4096]{1,0:T(8,128)(2,1)S(1)} all-gather(bf16[32,512]{1,0:T(8,128)(2,1)S(1)} %convert_select_fusion.2), channel_id=1, replica_groups=mesh['sec'=4,'bond'=8] {'bond'}, dimensions={1}, use_global_device_ids=true | all-gather | bytes 294912 | tf_op jit(solution)/shard_map/while/body/eval_jaxpr/all_gather | solution.py:86
  41.5 8.8 %convolution_multiply_fusion.3 = f32[32,2048]{1,0:T(8,128)S(1)} fusion(bf16[32,4096]{1,0:T(8,128)(2,1)S(1)} %all_gather.26, bf16[4096,2048]{1,0:T(8,128)(2,1)} %get-tuple-element.446, f32[32]{0:T(128)S(1)} %broadcast_select_fusion.4), kind=kOutput, calls=%fused_computation.1.clone.1 | convolution fusion | flops 536936448 | bytes 17301632 | tf_op jit(solution)/shard_map/while/body/eval_jaxpr/dot_general | solution.py:75
  51.7 3.9 %collective-permute-start = (bf16[32,512]{1,0:T(8,128)(2,1)S(1)}, bf16[32,512]{1,0:T(8,128)(2,1)S(1)}, u32[]{:S(2)}, u32[]{:S(2)}) collective-permute-start(bf16[32,512]{1,0:T(8,128)(2,1)S(1)} %get-tuple-element.395), channel_id=1, source_target_pairs={{0,8},{8,16},{16,24},{1,9},{9,17},{17,25},{2,10},{10,18},{18,26},{... | collective-permute-start | bytes 98312 | tf_op jit(solution)/shard_map/while/body/eval_jaxpr/ppermute | solution.py:14
  55.7 12.8 %all-gather.4 = f32[8,32,4]{1,2,0:T(4,128)S(1)} all-gather(f32[1,32,4]{1,2,0:T(4,128)S(1)} %bitcast.36), channel_id=2, replica_groups=mesh['sec'=4,'bond'=8] {'bond'}, dimensions={0}, use_global_device_ids=true | all-gather | bytes 4608 | tf_op jit(solution)/shard_map/while/body/eval_jaxpr/all_gather | solution.py:92
  68.8 3.4 collective-permute-start.1
  72.1 1.3 collective-permute-done.1
  74.2 14.2 %all_gather.26 = bf16[32,4096]{1,0:T(8,128)(2,1)S(1)} all-gather(bf16[32,512]{1,0:T(8,128)(2,1)S(1)} %convert_select_fusion.2), channel_id=1, replica_groups=mesh['sec'=4,'bond'=8] {'bond'}, dimensions={1}, use_global_device_ids=true | all-gather | bytes 294912 | tf_op jit(solution)/shard_map/while/body/eval_jaxpr/all_gather | solution.py:86
  88.4 8.8 %convolution_multiply_fusion.3 = f32[32,2048]{1,0:T(8,128)S(1)} fusion(bf16[32,4096]{1,0:T(8,128)(2,1)S(1)} %all_gather.26, bf16[4096,2048]{1,0:T(8,128)(2,1)} %get-tuple-element.446, f32[32]{0:T(128)S(1)} %broadcast_select_fusion.4), kind=kOutput, calls=%fused_computation.1.clone.1 | convolution fusion | flops 536936448 | bytes 17301632 | tf_op jit(solution)/shard_map/while/body/eval_jaxpr/dot_general | solution.py:75
  98.6 4.2 %collective-permute-start = (bf16[32,512]{1,0:T(8,128)(2,1)S(1)}, bf16[32,512]{1,0:T(8,128)(2,1)S(1)}, u32[]{:S(2)}, u32[]{:S(2)}) collective-permute-start(bf16[32,512]{1,0:T(8,128)(2,1)S(1)} %get-tuple-element.395), channel_id=1, source_target_pairs={{0,8},{8,16},{16,24},{1,9},{9,17},{17,25},{2,10},{10,18},{18,26},{... | collective-permute-start | bytes 98312 | tf_op jit(solution)/shard_map/while/body/eval_jaxpr/ppermute | solution.py:14
  102.8 12.8 %all-gather.4 = f32[8,32,4]{1,2,0:T(4,128)S(1)} all-gather(f32[1,32,4]{1,2,0:T(4,128)S(1)} %bitcast.36), channel_id=2, replica_groups=mesh['sec'=4,'bond'=8] {'bond'}, dimensions={0}, use_global_device_ids=true | all-gather | bytes 4608 | tf_op jit(solution)/shard_map/while/body/eval_jaxpr/all_gather | solution.py:92
  115.9 4.3 %collective-permute-start.1 = (f32[32]{0:T(128)S(1)}, f32[32]{0:T(128)S(1)}, u32[]{:S(2)}, u32[]{:S(2)}) collective-permute-start(f32[32]{0:T(128)S(1)} %get-tuple-element.399), channel_id=1, source_target_pairs={{0,8},{8,16},{16,24},{1,9},{9,17},{17,25},{2,10},{10,18},{18,26},{... | collective-permute-start | bytes 392 | tf_op jit(solution)/shard_map/while/body/eval_jaxpr/ppermute | solution.py:14
  120.1 1.3 collective-permute-done.1
  122.2 14.2 %all_gather.26 = bf16[32,4096]{1,0:T(8,128)(2,1)S(1)} all-gather(bf16[32,512]{1,0:T(8,128)(2,1)S(1)} %convert_select_fusion.2), channel_id=1, replica_groups=mesh['sec'=4,'bond'=8] {'bond'}, dimensions={1}, use_global_device_ids=true | all-gather | bytes 294912 | tf_op jit(solution)/shard_map/while/body/eval_jaxpr/all_gather | solution.py:86
  136.4 8.8 %convolution_multiply_fusion.3 = f32[32,2048]{1,0:T(8,128)S(1)} fusion(bf16[32,4096]{1,0:T(8,128)(2,1)S(1)} %all_gather.26, bf16[4096,2048]{1,0:T(8,128)(2,1)} %get-tuple-element.446, f32[32]{0:T(128)S(1)} %broadcast_select_fusion.4), kind=kOutput, calls=%fused_computation.1.clone.1 | convolution fusion | flops 536936448 | bytes 17301632 | tf_op jit(solution)/shard_map/while/body/eval_jaxpr/dot_general | solution.py:75
  145.8 0.8 multiply_reduce_fusion.3
  146.6 4.2 %collective-permute-start = (bf16[32,512]{1,0:T(8,128)(2,1)S(1)}, bf16[32,512]{1,0:T(8,128)(2,1)S(1)}, u32[]{:S(2)}, u32[]{:S(2)}) collective-permute-start(bf16[32,512]{1,0:T(8,128)(2,1)S(1)} %get-tuple-element.395), channel_id=1, source_target_pairs={{0,8},{8,16},{16,24},{1,9},{9,17},{17,25},{2,10},{10,18},{18,26},{... | collective-permute-start | bytes 98312 | tf_op jit(solution)/shard_map/while/body/eval_jaxpr/ppermute | solution.py:14
  150.8 12.8 %all-gather.4 = f32[8,32,4]{1,2,0:T(4,128)S(1)} all-gather(f32[1,32,4]{1,2,0:T(4,128)S(1)} %bitcast.36), channel_id=2, replica_groups=mesh['sec'=4,'bond'=8] {'bond'}, dimensions={0}, use_global_device_ids=true | all-gather | bytes 4608 | tf_op jit(solution)/shard_map/while/body/eval_jaxpr/all_gather | solution.py:92
  163.9 2.8 collective-permute-start.1
  166.7 1.3 collective-permute-done.1
  168.8 14.2 %all_gather.26 = bf16[32,4096]{1,0:T(8,128)(2,1)S(1)} all-gather(bf16[32,512]{1,0:T(8,128)(2,1)S(1)} %convert_select_fusion.2), channel_id=1, replica_groups=mesh['sec'=4,'bond'=8] {'bond'}, dimensions={1}, use_global_device_ids=true | all-gather | bytes 294912 | tf_op jit(solution)/shard_map/while/body/eval_jaxpr/all_gather | solution.py:86
  183.0 8.8 %convolution_multiply_fusion.3 = f32[32,2048]{1,0:T(8,128)S(1)} fusion(bf16[32,4096]{1,0:T(8,128)(2,1)S(1)} %all_gather.26, bf16[4096,2048]{1,0:T(8,128)(2,1)} %get-tuple-element.446, f32[32]{0:T(128)S(1)} %broadcast_select_fusion.4), kind=kOutput, calls=%fused_computation.1.clone.1 | convolution fusion | flops 536936448 | bytes 17301632 | tf_op jit(solution)/shard_map/while/body/eval_jaxpr/dot_general | solution.py:75
  192.3 0.8 multiply_reduce_fusion.3
  193.2 4.2 %collective-permute-start = (bf16[32,512]{1,0:T(8,128)(2,1)S(1)}, bf16[32,512]{1,0:T(8,128)(2,1)S(1)}, u32[]{:S(2)}, u32[]{:S(2)}) collective-permute-start(bf16[32,512]{1,0:T(8,128)(2,1)S(1)} %get-tuple-element.395), channel_id=1, source_target_pairs={{0,8},{8,16},{16,24},{1,9},{9,17},{17,25},{2,10},{10,18},{18,26},{... | collective-permute-start | bytes 98312 | tf_op jit(solution)/shard_map/while/body/eval_jaxpr/ppermute | solution.py:14
  197.4 12.8 %all-gather.4 = f32[8,32,4]{1,2,0:T(4,128)S(1)} all-gather(f32[1,32,4]{1,2,0:T(4,128)S(1)} %bitcast.36), channel_id=2, replica_groups=mesh['sec'=4,'bond'=8] {'bond'}, dimensions={0}, use_global_device_ids=true | all-gather | bytes 4608 | tf_op jit(solution)/shard_map/while/body/eval_jaxpr/all_gather | solution.py:92
  210.5 2.8 collective-permute-start.1
  213.3 1.3 collective-permute-done.1
  215.3 14.2 %all_gather.26 = bf16[32,4096]{1,0:T(8,128)(2,1)S(1)} all-gather(bf16[32,512]{1,0:T(8,128)(2,1)S(1)} %convert_select_fusion.2), channel_id=1, replica_groups=mesh['sec'=4,'bond'=8] {'bond'}, dimensions={1}, use_global_device_ids=true | all-gather | bytes 294912 | tf_op jit(solution)/shard_map/while/body/eval_jaxpr/all_gather | solution.py:86
  229.5 8.8 %convolution_multiply_fusion.3 = f32[32,2048]{1,0:T(8,128)S(1)} fusion(bf16[32,4096]{1,0:T(8,128)(2,1)S(1)} %all_gather.26, bf16[4096,2048]{1,0:T(8,128)(2,1)} %get-tuple-element.446, f32[32]{0:T(128)S(1)} %broadcast_select_fusion.4), kind=kOutput, calls=%fused_computation.1.clone.1 | convolution fusion | flops 536936448 | bytes 17301632 | tf_op jit(solution)/shard_map/while/body/eval_jaxpr/dot_general | solution.py:75
  239.7 4.2 %collective-permute-start = (bf16[32,512]{1,0:T(8,128)(2,1)S(1)}, bf16[32,512]{1,0:T(8,128)(2,1)S(1)}, u32[]{:S(2)}, u32[]{:S(2)}) collective-permute-start(bf16[32,512]{1,0:T(8,128)(2,1)S(1)} %get-tuple-element.395), channel_id=1, source_target_pairs={{0,8},{8,16},{16,24},{1,9},{9,17},{17,25},{2,10},{10,18},{18,26},{... | collective-permute-start | bytes 98312 | tf_op jit(solution)/shard_map/while/body/eval_jaxpr/ppermute | solution.py:14
  244.0 12.8 %all-gather.4 = f32[8,32,4]{1,2,0:T(4,128)S(1)} all-gather(f32[1,32,4]{1,2,0:T(4,128)S(1)} %bitcast.36), channel_id=2, replica_groups=mesh['sec'=4,'bond'=8] {'bond'}, dimensions={0}, use_global_device_ids=true | all-gather | bytes 4608 | tf_op jit(solution)/shard_map/while/body/eval_jaxpr/all_gather | solution.py:92
  257.0 2.8 collective-permute-start.1
  259.8 1.3 collective-permute-done.1
  261.9 14.2 %all_gather.26 = bf16[32,4096]{1,0:T(8,128)(2,1)S(1)} all-gather(bf16[32,512]{1,0:T(8,128)(2,1)S(1)} %convert_select_fusion.2), channel_id=1, replica_groups=mesh['sec'=4,'bond'=8] {'bond'}, dimensions={1}, use_global_device_ids=true | all-gather | bytes 294912 | tf_op jit(solution)/shard_map/while/body/eval_jaxpr/all_gather | solution.py:86
  276.1 8.8 %convolution_multiply_fusion.3 = f32[32,2048]{1,0:T(8,128)S(1)} fusion(bf16[32,4096]{1,0:T(8,128)(2,1)S(1)} %all_gather.26, bf16[4096,2048]{1,0:T(8,128)(2,1)} %get-tuple-element.446, f32[32]{0:T(128)S(1)} %broadcast_select_fusion.4), kind=kOutput, calls=%fused_computation.1.clone.1 | convolution fusion | flops 536936448 | bytes 17301632 | tf_op jit(solution)/shard_map/while/body/eval_jaxpr/dot_general | solution.py:75
  286.3 4.2 %collective-permute-start = (bf16[32,512]{1,0:T(8,128)(2,1)S(1)}, bf16[32,512]{1,0:T(8,128)(2,1)S(1)}, u32[]{:S(2)}, u32[]{:S(2)}) collective-permute-start(bf16[32,512]{1,0:T(8,128)(2,1)S(1)} %get-tuple-element.395), channel_id=1, source_target_pairs={{0,8},{8,16},{16,24},{1,9},{9,17},{17,25},{2,10},{10,18},{18,26},{... | collective-permute-start | bytes 98312 | tf_op jit(solution)/shard_map/while/body/eval_jaxpr/ppermute | solution.py:14
  290.6 12.8 %all-gather.4 = f32[8,32,4]{1,2,0:T(4,128)S(1)} all-gather(f32[1,32,4]{1,2,0:T(4,128)S(1)} %bitcast.36), channel_id=2, replica_groups=mesh['sec'=4,'bond'=8] {'bond'}, dimensions={0}, use_global_device_ids=true | all-gather | bytes 4608 | tf_op jit(solution)/shard_map/while/body/eval_jaxpr/all_gather | solution.py:92
  303.6 2.8 collective-permute-start.1
  306.4 1.3 collective-permute-done.1
  308.5 14.2 %all_gather.26 = bf16[32,4096]{1,0:T(8,128)(2,1)S(1)} all-gather(bf16[32,512]{1,0:T(8,128)(2,1)S(1)} %convert_select_fusion.2), channel_id=1, replica_groups=mesh['sec'=4,'bond'=8] {'bond'}, dimensions={1}, use_global_device_ids=true | all-gather | bytes 294912 | tf_op jit(solution)/shard_map/while/body/eval_jaxpr/all_gather | solution.py:86
  322.7 8.8 %convolution_multiply_fusion.3 = f32[32,2048]{1,0:T(8,128)S(1)} fusion(bf16[32,4096]{1,0:T(8,128)(2,1)S(1)} %all_gather.26, bf16[4096,2048]{1,0:T(8,128)(2,1)} %get-tuple-element.446, f32[32]{0:T(128)S(1)} %broadcast_select_fusion.4), kind=kOutput, calls=%fused_computation.1.clone.1 | convolution fusion | flops 536936448 | bytes 17301632 | tf_op jit(solution)/shard_map/while/body/eval_jaxpr/dot_general | solution.py:75
  332.9 4.2 %collective-permute-start = (bf16[32,512]{1,0:T(8,128)(2,1)S(1)}, bf16[32,512]{1,0:T(8,128)(2,1)S(1)}, u32[]{:S(2)}, u32[]{:S(2)}) collective-permute-start(bf16[32,512]{1,0:T(8,128)(2,1)S(1)} %get-tuple-element.395), channel_id=1, source_target_pairs={{0,8},{8,16},{16,24},{1,9},{9,17},{17,25},{2,10},{10,18},{18,26},{... | collective-permute-start | bytes 98312 | tf_op jit(solution)/shard_map/while/body/eval_jaxpr/ppermute | solution.py:14
  337.1 12.8 %all-gather.4 = f32[8,32,4]{1,2,0:T(4,128)S(1)} all-gather(f32[1,32,4]{1,2,0:T(4,128)S(1)} %bitcast.36), channel_id=2, replica_groups=mesh['sec'=4,'bond'=8] {'bond'}, dimensions={0}, use_global_device_ids=true | all-gather | bytes 4608 | tf_op jit(solution)/shard_map/while/body/eval_jaxpr/all_gather | solution.py:92
  350.2 2.8 collective-permute-start.1
  353.0 1.3 collective-permute-done.1
  (126 shorter events, 19.3 us)
Async XLA Ops:
  3.7 22.1 %all-to-all-start = ((f32[2,32,4]{1,0,2:T(2,128)}), f32[2,32,4]{1,0,2:T(2,128)S(1)}, u32[]{:S(2)}, u32[]{:S(2)}) async-start(f32[2,32,4]{1,0,2:T(2,128)} %copy.11), calls=%async_computation | async-start | bytes 8192 | tf_op jit(solution)/shard_map/all_to_all | solution.py:65
  8.8 17.2 %copy-start.2 = (f32[4,4,7]{2,1,0:T(4,128)S(1)}, f32[4,4,7]{2,1,0:T(4,128)}, u32[]{:S(2)}) copy-start(f32[4,4,7]{2,1,0:T(4,128)} %constant.99.clone) | copy-start | bytes 1348
  51.7 21.7 %collective-permute-start = (bf16[32,512]{1,0:T(8,128)(2,1)S(1)}, bf16[32,512]{1,0:T(8,128)(2,1)S(1)}, u32[]{:S(2)}, u32[]{:S(2)}) collective-permute-start(bf16[32,512]{1,0:T(8,128)(2,1)S(1)} %get-tuple-element.395), channel_id=1, source_target_pairs={{0,8},{8,16},{16,24},{1,9},{9,17},{17,25},{2,10},{10,18},{18,26},{... | collective-permute-start | bytes 98312 | tf_op jit(solution)/shard_map/while/body/eval_jaxpr/ppermute | solution.py:14
  68.8 4.7 %collective-permute-start.1 = (f32[32]{0:T(128)S(1)}, f32[32]{0:T(128)S(1)}, u32[]{:S(2)}, u32[]{:S(2)}) collective-permute-start(f32[32]{0:T(128)S(1)} %get-tuple-element.399), channel_id=1, source_target_pairs={{0,8},{8,16},{16,24},{1,9},{9,17},{17,25},{2,10},{10,18},{18,26},{... | collective-permute-start | bytes 392 | tf_op jit(solution)/shard_map/while/body/eval_jaxpr/ppermute | solution.py:14
  98.6 22.8 %collective-permute-start = (bf16[32,512]{1,0:T(8,128)(2,1)S(1)}, bf16[32,512]{1,0:T(8,128)(2,1)S(1)}, u32[]{:S(2)}, u32[]{:S(2)}) collective-permute-start(bf16[32,512]{1,0:T(8,128)(2,1)S(1)} %get-tuple-element.395), channel_id=1, source_target_pairs={{0,8},{8,16},{16,24},{1,9},{9,17},{17,25},{2,10},{10,18},{18,26},{... | collective-permute-start | bytes 98312 | tf_op jit(solution)/shard_map/while/body/eval_jaxpr/ppermute | solution.py:14
  115.9 5.5 %collective-permute-start.1 = (f32[32]{0:T(128)S(1)}, f32[32]{0:T(128)S(1)}, u32[]{:S(2)}, u32[]{:S(2)}) collective-permute-start(f32[32]{0:T(128)S(1)} %get-tuple-element.399), channel_id=1, source_target_pairs={{0,8},{8,16},{16,24},{1,9},{9,17},{17,25},{2,10},{10,18},{18,26},{... | collective-permute-start | bytes 392 | tf_op jit(solution)/shard_map/while/body/eval_jaxpr/ppermute | solution.py:14
  146.6 21.4 %collective-permute-start = (bf16[32,512]{1,0:T(8,128)(2,1)S(1)}, bf16[32,512]{1,0:T(8,128)(2,1)S(1)}, u32[]{:S(2)}, u32[]{:S(2)}) collective-permute-start(bf16[32,512]{1,0:T(8,128)(2,1)S(1)} %get-tuple-element.395), channel_id=1, source_target_pairs={{0,8},{8,16},{16,24},{1,9},{9,17},{17,25},{2,10},{10,18},{18,26},{... | collective-permute-start | bytes 98312 | tf_op jit(solution)/shard_map/while/body/eval_jaxpr/ppermute | solution.py:14
  163.9 4.1 %collective-permute-start.1 = (f32[32]{0:T(128)S(1)}, f32[32]{0:T(128)S(1)}, u32[]{:S(2)}, u32[]{:S(2)}) collective-permute-start(f32[32]{0:T(128)S(1)} %get-tuple-element.399), channel_id=1, source_target_pairs={{0,8},{8,16},{16,24},{1,9},{9,17},{17,25},{2,10},{10,18},{18,26},{... | collective-permute-start | bytes 392 | tf_op jit(solution)/shard_map/while/body/eval_jaxpr/ppermute | solution.py:14
  193.2 21.4 %collective-permute-start = (bf16[32,512]{1,0:T(8,128)(2,1)S(1)}, bf16[32,512]{1,0:T(8,128)(2,1)S(1)}, u32[]{:S(2)}, u32[]{:S(2)}) collective-permute-start(bf16[32,512]{1,0:T(8,128)(2,1)S(1)} %get-tuple-element.395), channel_id=1, source_target_pairs={{0,8},{8,16},{16,24},{1,9},{9,17},{17,25},{2,10},{10,18},{18,26},{... | collective-permute-start | bytes 98312 | tf_op jit(solution)/shard_map/while/body/eval_jaxpr/ppermute | solution.py:14
  210.5 4.1 %collective-permute-start.1 = (f32[32]{0:T(128)S(1)}, f32[32]{0:T(128)S(1)}, u32[]{:S(2)}, u32[]{:S(2)}) collective-permute-start(f32[32]{0:T(128)S(1)} %get-tuple-element.399), channel_id=1, source_target_pairs={{0,8},{8,16},{16,24},{1,9},{9,17},{17,25},{2,10},{10,18},{18,26},{... | collective-permute-start | bytes 392 | tf_op jit(solution)/shard_map/while/body/eval_jaxpr/ppermute | solution.py:14
  239.7 21.4 %collective-permute-start = (bf16[32,512]{1,0:T(8,128)(2,1)S(1)}, bf16[32,512]{1,0:T(8,128)(2,1)S(1)}, u32[]{:S(2)}, u32[]{:S(2)}) collective-permute-start(bf16[32,512]{1,0:T(8,128)(2,1)S(1)} %get-tuple-element.395), channel_id=1, source_target_pairs={{0,8},{8,16},{16,24},{1,9},{9,17},{17,25},{2,10},{10,18},{18,26},{... | collective-permute-start | bytes 98312 | tf_op jit(solution)/shard_map/while/body/eval_jaxpr/ppermute | solution.py:14
  257.0 4.1 %collective-permute-start.1 = (f32[32]{0:T(128)S(1)}, f32[32]{0:T(128)S(1)}, u32[]{:S(2)}, u32[]{:S(2)}) collective-permute-start(f32[32]{0:T(128)S(1)} %get-tuple-element.399), channel_id=1, source_target_pairs={{0,8},{8,16},{16,24},{1,9},{9,17},{17,25},{2,10},{10,18},{18,26},{... | collective-permute-start | bytes 392 | tf_op jit(solution)/shard_map/while/body/eval_jaxpr/ppermute | solution.py:14
  286.3 21.4 %collective-permute-start = (bf16[32,512]{1,0:T(8,128)(2,1)S(1)}, bf16[32,512]{1,0:T(8,128)(2,1)S(1)}, u32[]{:S(2)}, u32[]{:S(2)}) collective-permute-start(bf16[32,512]{1,0:T(8,128)(2,1)S(1)} %get-tuple-element.395), channel_id=1, source_target_pairs={{0,8},{8,16},{16,24},{1,9},{9,17},{17,25},{2,10},{10,18},{18,26},{... | collective-permute-start | bytes 98312 | tf_op jit(solution)/shard_map/while/body/eval_jaxpr/ppermute | solution.py:14
  303.6 4.1 %collective-permute-start.1 = (f32[32]{0:T(128)S(1)}, f32[32]{0:T(128)S(1)}, u32[]{:S(2)}, u32[]{:S(2)}) collective-permute-start(f32[32]{0:T(128)S(1)} %get-tuple-element.399), channel_id=1, source_target_pairs={{0,8},{8,16},{16,24},{1,9},{9,17},{17,25},{2,10},{10,18},{18,26},{... | collective-permute-start | bytes 392 | tf_op jit(solution)/shard_map/while/body/eval_jaxpr/ppermute | solution.py:14
  332.9 21.4 %collective-permute-start = (bf16[32,512]{1,0:T(8,128)(2,1)S(1)}, bf16[32,512]{1,0:T(8,128)(2,1)S(1)}, u32[]{:S(2)}, u32[]{:S(2)}) collective-permute-start(bf16[32,512]{1,0:T(8,128)(2,1)S(1)} %get-tuple-element.395), channel_id=1, source_target_pairs={{0,8},{8,16},{16,24},{1,9},{9,17},{17,25},{2,10},{10,18},{18,26},{... | collective-permute-start | bytes 98312 | tf_op jit(solution)/shard_map/while/body/eval_jaxpr/ppermute | solution.py:14
  350.2 4.1 %collective-permute-start.1 = (f32[32]{0:T(128)S(1)}, f32[32]{0:T(128)S(1)}, u32[]{:S(2)}, u32[]{:S(2)}) collective-permute-start(f32[32]{0:T(128)S(1)} %get-tuple-element.399), channel_id=1, source_target_pairs={{0,8},{8,16},{16,24},{1,9},{9,17},{17,25},{2,10},{10,18},{18,26},{... | collective-permute-start | bytes 392 | tf_op jit(solution)/shard_map/while/body/eval_jaxpr/ppermute | solution.py:14
  354.3 0.5 copy-start
  354.3 0.5 copy-start.1
